TPU v7x, 512 devices: a whole 4x4x16 slice. The times are simulated.
512 devices in a mesh: row: 16 (over z), col: 32 (over x, y, core).
Axes of the slice: x: 4, y: 4, z: 16, core: 2. Of those that a mesh axis runs over, the one named last changes fastest.
Arguments:
- rhs_panels: float32 [3, 16, 32, 64, 256], P(None, 'row', 'col'), may hold values from -6 to 6
- inverse_diag: bfloat16 [3, 16, 32, 256, 256], P(None, 'row', 'col'), may hold values from -0.375 to 0.375
- factor_blocks: bfloat16 [3, 16, 320, 256, 256], P(None, 'row', 'col'), may hold values from -0.078125 to 0.078125
- block_target: int32 [3, 16, 320], P(None, 'row', 'col'), may hold values from 0 to 15, as said below
- block_source: int32 [3, 16, 320], P(None, 'row', 'col'), may hold values from 0 to 31, as said below
Outputs:
- solution: float32 [3, 16, 32, 64, 256], P(None, 'row', 'col')
Inputs may be any that keep to these rules, and one draw needn't show every extreme that they name: (block_target[p, r, q] - r) modulo 16 is below 2, or equals 8, or equals 15; each of 1, 8 and 15 occurs. (block_source[p, r, q] - q // 10) modulo 32 is below 2, or equals 16, or equals 31; each of 1, 16 and 31 occurs.
All inputs are finite; a program needn't handle non-finite values.
Results may differ from a plain program's by a relative error of at most 0.014.
Values may be sent and summed in bfloat16 or wider, within the bound.
No kernel may reach another device: no remote copies, remote signals or barrier semaphores. Data moves between devices by JAX's collectives and lax.ppermute only.
A program may use at most 64 MiB of HBM per device.

v0:
```python
import jax
import jax.numpy as jnp
from jax import lax
from jax.sharding import PartitionSpec as P

WINDOW = 2


def from_behind(value, axis, steps):
    count = lax.axis_size(axis)
    pairs = [(source, (source + steps) % count) for source in range(count)]
    return lax.ppermute(value, axis, pairs)


def laid_out(pieces, dim):
    dims = list(pieces.shape[1:])
    dims[dim] *= pieces.shape[0]
    return jnp.moveaxis(pieces, 0, dim).reshape(dims)


def from_everyone(value, axis):
    count = lax.axis_size(axis)
    return lax.all_to_all(
        jnp.broadcast_to(value[None], (count, *value.shape)), axis, 0, 0, tiled=True
    )


def collect(value, axis, dim):
    return laid_out(from_everyone(value, axis), dim)


def pair_table(levels):
    return [
        (target_lvl, source_lvl)
        for target_lvl in range(1, levels)
        for source_lvl in range(target_lvl)
    ]


def offset_choices(window, count):
    values = sorted(set(list(range(window)) + [count // 2, count - 1]))
    return values


def offset_places(offsets, values):
    places = jnp.zeros(offsets.shape, jnp.int32)
    for position, value in enumerate(values):
        places = places + jnp.where(offsets == value, position, 0).astype(jnp.int32)
    return places


def spread_rows(indices, row_count, products):
    onehot = (indices[None, :] == jnp.arange(row_count, dtype=jnp.int32)[:, None]).astype(
        jnp.float32
    )
    flattened = products.reshape(products.shape[0], -1)
    summed = jnp.dot(
        onehot, flattened, precision=lax.Precision.HIGHEST, preferred_element_type=jnp.float32
    )
    return summed.reshape((row_count,) + products.shape[1:])


def deliver_rows(partial_value, values):
    summed = partial_value[0].astype(jnp.bfloat16).astype(jnp.float32)
    for position in range(1, partial_value.shape[0]):
        moved = from_behind(partial_value[position].astype(jnp.bfloat16), "row", values[position])
        summed = summed + moved.astype(jnp.float32)
    return summed


def deliver_cols(partial_value, values):
    summed = partial_value[0].astype(jnp.bfloat16).astype(jnp.float32)
    for position in range(1, partial_value.shape[0]):
        moved = from_behind(partial_value[position].astype(jnp.bfloat16), "col", values[position])
        summed = summed + moved.astype(jnp.float32)
    return summed


def shards(rhs_panels, inverse_diag, factor_blocks, block_target, block_source):
    levels = rhs_panels.shape[0]
    row_devices = lax.axis_size("row")
    col_devices = lax.axis_size("col")
    pair_list = pair_table(levels)
    blocks = factor_blocks[:, 0]
    targets = block_target[:, 0]
    sources = block_source[:, 0]
    row_values = offset_choices(WINDOW, row_devices)
    col_values = offset_choices(WINDOW, col_devices)
    row_keys = offset_places((targets - lax.axis_index("row")) % row_devices, row_values)
    col_keys = offset_places((sources - lax.axis_index("col")) % col_devices, col_values)
    row_width = len(row_values)
    col_width = len(col_values)
    forward = []
    gathered = {}
    for current in range(levels):
        residual = rhs_panels[current, 0, 0]
        if current > 0:
            partial_value = jnp.zeros((row_width,) + residual.shape, jnp.float32)
            for pair_idx, pair_info in enumerate(pair_list):
                if pair_info[0] == current:
                    picked = jnp.take(gathered[pair_info[1]], sources[pair_idx], axis=0)
                    products = jnp.einsum(
                        "snb,sab->sna", picked, blocks[pair_idx], preferred_element_type=jnp.float32
                    )
                    partial_value = partial_value + spread_rows(
                        row_keys[pair_idx], row_width, products
                    )
            summed = deliver_rows(partial_value, row_values)
            residual = residual - summed
        reduced = residual.astype(jnp.bfloat16)
        panel_now = lax.dot_general(
            reduced,
            inverse_diag[current, 0, 0],
            (((1,), (1,)), ((), ())),
            preferred_element_type=jnp.float32,
        )
        forward.append(panel_now)
        if current < levels - 1:
            outgoing = panel_now.astype(jnp.bfloat16)[None]
            gathered[current] = collect(outgoing, "col", 0)
    solutions = [None] * levels
    gathered_back = {}
    for current in reversed(range(levels)):
        residual = forward[current]
        if current < levels - 1:
            partial_value = jnp.zeros((col_width,) + residual.shape, jnp.float32)
            for pair_idx, pair_info in enumerate(pair_list):
                if pair_info[1] == current:
                    picked = jnp.take(gathered_back[pair_info[0]], targets[pair_idx], axis=0)
                    products = jnp.einsum(
                        "snb,sba->sna", picked, blocks[pair_idx], preferred_element_type=jnp.float32
                    )
                    partial_value = partial_value + spread_rows(
                        col_keys[pair_idx], col_width, products
                    )
            summed = deliver_cols(partial_value, col_values)
            residual = residual - summed
        reduced = residual.astype(jnp.bfloat16)
        answer = jnp.dot(reduced, inverse_diag[current, 0, 0], preferred_element_type=jnp.float32)
        solutions[current] = answer
        if current > 0:
            outgoing = answer.astype(jnp.bfloat16)[None]
            gathered_back[current] = lax.all_gather(outgoing, "row", axis=0, tiled=True)
    return jnp.stack(solutions)[:, None, None]


def solution(mesh):
    placed = (
        P(None, "row", "col", None, None),
        P(None, "row", "col", None, None),
        P(None, "row", "col", None, None),
        P(None, "row", "col"),
        P(None, "row", "col"),
    )
    return jax.shard_map(
        shards,
        mesh=mesh,
        in_specs=placed,
        out_specs=P(None, "row", "col", None, None),
        check_vma=False,
    )
```

profile of v0, /device:TPU:32, one launch (start us, length us, event | category | flops | bytes accessed | tf_op | source)
XLA Modules:
  0.0 198.4 jit_solution(18369573394711938383)
XLA Ops:
  0.0 1.1 fusion.101
  1.1 1.1 broadcast_in_dim.67
  2.2 7.3 %all-to-all-start = ((bf16[32,1,64,256]{3,2,1,0:T(8,128)(2,1)}), bf16[32,1,64,256]{3,2,1,0:T(8,128)(2,1)S(1)}, u32[]{:S(2)}, u32[]{:S(2)}) async-start(bf16[32,1,64,256]{3,2,1,0:T(8,128)(2,1)} %broadcast_in_dim.67), calls=%async_computation | async-start | bytes 2097152 | tf_op jit(solution)/shard_map/all_to_all | solution.py:23
  9.6 0.7 compare_and_fusion.3
  10.3 0.7 broadcast_subtract_fusion.1
  10.9 0.7 broadcast_subtract_fusion
  11.6 0.7 compare_and_fusion.1
  12.4 14.0 %all-to-all-done = bf16[32,1,64,256]{3,2,1,0:T(8,128)(2,1)S(1)} async-done(((bf16[32,1,64,256]{3,2,1,0:T(8,128)(2,1)}), bf16[32,1,64,256]{3,2,1,0:T(8,128)(2,1)S(1)}, u32[]{:S(2)}, u32[]{:S(2)}) %all-to-all-start) | async-done | bytes 1048608 | tf_op jit(solution)/shard_map/all_to_all | solution.py:23
  26.3 0.6 gather_fusion
  26.9 1.9 fusion.10
  28.8 0.1 pad.9
  28.9 0.6 copy.42
  29.5 0.5 convolution_convert_fusion.1
  30.0 0.6 slice_reduce_fusion.5
  30.6 14.8 %collective-permute-start.1 = (bf16[64,256]{1,0:T(8,128)(2,1)S(1)}, bf16[64,256]{1,0:T(8,128)(2,1)S(1)}, u32[]{:S(2)}, u32[]{:S(2)}) collective-permute-start(bf16[64,256]{1,0:T(8,128)(2,1)S(1)} %convert_element_type.159), channel_id=1, source_target_pairs={{0,256},{32,288},{64,320},{96,352},{128,384},{160,416},{192,448},{... | collective-permute-start | bytes 98312 | tf_op jit(solution)/shard_map/ppermute | solution.py:12
  45.5 2.9 %collective-permute-start.2 = (bf16[64,256]{1,0:T(8,128)(2,1)S(1)}, bf16[64,256]{1,0:T(8,128)(2,1)S(1)}, u32[]{:S(2)}, u32[]{:S(2)}) collective-permute-start(bf16[64,256]{1,0:T(8,128)(2,1)S(1)} %convert_element_type.161), channel_id=1, source_target_pairs={{0,480},{32,0},{64,32},{96,64},{128,96},{160,128},{192,160},{224,1... | collective-permute-start | bytes 98312 | tf_op jit(solution)/shard_map/ppermute | solution.py:12
  48.4 2.9 %collective-permute-start = (bf16[64,256]{1,0:T(8,128)(2,1)S(1)}, bf16[64,256]{1,0:T(8,128)(2,1)S(1)}, u32[]{:S(2)}, u32[]{:S(2)}) collective-permute-start(bf16[64,256]{1,0:T(8,128)(2,1)S(1)} %convert_element_type.157), channel_id=1, source_target_pairs={{0,32},{32,64},{64,96},{96,128},{128,160},{160,192},{192,224},{224... | collective-permute-start | bytes 98312 | tf_op jit(solution)/shard_map/ppermute | solution.py:12
  51.3 0.2 fusion.62
  51.6 2.6 %collective-permute-done = bf16[64,256]{1,0:T(8,128)(2,1)S(1)} collective-permute-done((bf16[64,256]{1,0:T(8,128)(2,1)S(1)}, bf16[64,256]{1,0:T(8,128)(2,1)S(1)}, u32[]{:S(2)}, u32[]{:S(2)}) %collective-permute-start) | collective-permute-done | bytes 32800 | tf_op jit(solution)/shard_map/ppermute | solution.py:12
  54.2 0.2 fusion.102
  54.4 1.1 broadcast_in_dim.68
  55.5 4.1 %all-to-all-start.1 = ((bf16[32,1,64,256]{3,2,1,0:T(8,128)(2,1)}), bf16[32,1,64,256]{3,2,1,0:T(8,128)(2,1)S(1)}, u32[]{:S(2)}, u32[]{:S(2)}) async-start(bf16[32,1,64,256]{3,2,1,0:T(8,128)(2,1)} %broadcast_in_dim.68), calls=%async_computation.1 | async-start | bytes 2097152 | tf_op jit(solution)/shard_map/all_to_all | solution.py:23
  59.6 0.6 gather_fusion.1
  60.2 1.8 fusion.6
  62.1 0.8 fusion.25
  62.9 13.5 %all-to-all-done.1 = bf16[32,1,64,256]{3,2,1,0:T(8,128)(2,1)S(1)} async-done(((bf16[32,1,64,256]{3,2,1,0:T(8,128)(2,1)}), bf16[32,1,64,256]{3,2,1,0:T(8,128)(2,1)S(1)}, u32[]{:S(2)}, u32[]{:S(2)}) %all-to-all-start.1) | async-done | bytes 1048608 | tf_op jit(solution)/shard_map/all_to_all | solution.py:23
  76.3 0.6 gather_fusion.2
  76.9 1.8 fusion.2
  78.8 0.8 fusion.18
  79.6 0.2 fusion.100
  79.9 6.3 %collective-permute-start.4 = (bf16[64,256]{1,0:T(8,128)(2,1)S(1)}, bf16[64,256]{1,0:T(8,128)(2,1)S(1)}, u32[]{:S(2)}, u32[]{:S(2)}) collective-permute-start(bf16[64,256]{1,0:T(8,128)(2,1)S(1)} %bitcast.224), channel_id=1, source_target_pairs={{0,256},{32,288},{64,320},{96,352},{128,384},{160,416},{192,448},{... | collective-permute-start | bytes 98312 | tf_op jit(solution)/shard_map/ppermute | solution.py:12
  86.2 5.1 %collective-permute-start.5 = (bf16[64,256]{1,0:T(8,128)(2,1)S(1)}, bf16[64,256]{1,0:T(8,128)(2,1)S(1)}, u32[]{:S(2)}, u32[]{:S(2)}) collective-permute-start(bf16[64,256]{1,0:T(8,128)(2,1)S(1)} %bitcast.223), channel_id=1, source_target_pairs={{0,480},{32,0},{64,32},{96,64},{128,96},{160,128},{192,160},{224,1... | collective-permute-start | bytes 98312 | tf_op jit(solution)/shard_map/ppermute | solution.py:12
  91.3 1.9 collective-permute-start.3
  93.3 1.1 collective-permute-done.4
  94.4 2.7 %collective-permute-done.3 = bf16[64,256]{1,0:T(8,128)(2,1)S(1)} collective-permute-done((bf16[64,256]{1,0:T(8,128)(2,1)S(1)}, bf16[64,256]{1,0:T(8,128)(2,1)S(1)}, u32[]{:S(2)}, u32[]{:S(2)}) %collective-permute-start.3) | collective-permute-done | bytes 32800 | tf_op jit(solution)/shard_map/ppermute | solution.py:12
  97.1 0.3 fusion.103
  97.5 30.1 %all-gather = bf16[1024,256]{1,0:T(8,128)(2,1)S(1)} all-gather(bf16[64,256]{1,0:T(8,128)(2,1)S(1)} %get-tuple-element.50), channel_id=2, replica_groups=mesh['row'=16,'col'=32] {'row'}, dimensions={0}, use_global_device_ids=true | all-gather | bytes 557056 | tf_op jit(solution)/shard_map/all_gather | solution.py:143
  127.5 0.6 gather_fusion.5
  128.1 0.6 gather_fusion.3
  128.7 1.7 fusion.4
  130.4 0.1 slice_bitcast_fusion
  130.5 1.7 fusion
  132.2 0.1 pad.12
  132.3 0.6 copy.47
  132.9 0.5 convolution_convert_fusion
  133.4 0.6 slice_reduce_fusion.2
  134.0 3.4 %collective-permute-start.7 = (bf16[64,256]{1,0:T(8,128)(2,1)S(1)}, bf16[64,256]{1,0:T(8,128)(2,1)S(1)}, u32[]{:S(2)}, u32[]{:S(2)}) collective-permute-start(bf16[64,256]{1,0:T(8,128)(2,1)S(1)} %convert_element_type.180), channel_id=1, source_target_pairs={{0,16},{1,17},{2,18},{3,19},{4,20},{5,21},{6,22},{7,23},{8,24},{9,... | collective-permute-start | bytes 98312 | tf_op jit(solution)/shard_map/ppermute | solution.py:12
  137.4 1.9 collective-permute-start.8
  139.3 2.4 %collective-permute-start.6 = (bf16[64,256]{1,0:T(8,128)(2,1)S(1)}, bf16[64,256]{1,0:T(8,128)(2,1)S(1)}, u32[]{:S(2)}, u32[]{:S(2)}) collective-permute-start(bf16[64,256]{1,0:T(8,128)(2,1)S(1)} %convert_element_type.178), channel_id=1, source_target_pairs={{0,1},{1,2},{2,3},{3,4},{4,5},{5,6},{6,7},{7,8},{8,9},{9,10},{10,1... | collective-permute-start | bytes 98312 | tf_op jit(solution)/shard_map/ppermute | solution.py:12
  141.8 0.8 fusion.20
  142.6 0.2 fusion.61
  142.8 5.1 %collective-permute-done.6 = bf16[64,256]{1,0:T(8,128)(2,1)S(1)} collective-permute-done((bf16[64,256]{1,0:T(8,128)(2,1)S(1)}, bf16[64,256]{1,0:T(8,128)(2,1)S(1)}, u32[]{:S(2)}, u32[]{:S(2)}) %collective-permute-start.6) | collective-permute-done | bytes 32800 | tf_op jit(solution)/shard_map/ppermute | solution.py:12
  147.9 0.1 fusion.108
  148.0 30.0 %all-gather.1 = bf16[1024,256]{1,0:T(8,128)(2,1)S(1)} all-gather(bf16[64,256]{1,0:T(8,128)(2,1)S(1)} %get-tuple-element.52), channel_id=3, replica_groups=mesh['row'=16,'col'=32] {'row'}, dimensions={0}, use_global_device_ids=true | all-gather | bytes 557056 | tf_op jit(solution)/shard_map/all_gather | solution.py:143
  178.1 0.6 gather_fusion.4
  178.6 1.7 fusion.8
  180.4 0.8 fusion.22
  181.2 0.1 fusion.39
  181.3 1.9 collective-permute-start.9
  183.2 7.0 %collective-permute-start.11 = (bf16[64,256]{1,0:T(8,128)(2,1)S(1)}, bf16[64,256]{1,0:T(8,128)(2,1)S(1)}, u32[]{:S(2)}, u32[]{:S(2)}) collective-permute-start(bf16[64,256]{1,0:T(8,128)(2,1)S(1)} %get-tuple-element.26), channel_id=1, source_target_pairs={{0,31},{1,0},{2,1},{3,2},{4,3},{5,4},{6,5},{7,6},{8,7},{9,8},{10,9... | collective-permute-start | bytes 98312 | tf_op jit(solution)/shard_map/ppermute | solution.py:12
  190.2 1.9 collective-permute-start.10
  192.2 5.4 %collective-permute-done.10 = bf16[64,256]{1,0:T(8,128)(2,1)S(1)} collective-permute-done((bf16[64,256]{1,0:T(8,128)(2,1)S(1)}, bf16[64,256]{1,0:T(8,128)(2,1)S(1)}, u32[]{:S(2)}, u32[]{:S(2)}) %collective-permute-start.10) | collective-permute-done | bytes 32800 | tf_op jit(solution)/shard_map/ppermute | solution.py:12
  197.5 0.2 convolution_bitcast_fusion
  197.7 0.7 maximum_bitcast_fusion
  (34 shorter events, 0.4 us)
Async XLA Ops:
  2.2 24.1 %all-to-all-start = ((bf16[32,1,64,256]{3,2,1,0:T(8,128)(2,1)}), bf16[32,1,64,256]{3,2,1,0:T(8,128)(2,1)S(1)}, u32[]{:S(2)}, u32[]{:S(2)}) async-start(bf16[32,1,64,256]{3,2,1,0:T(8,128)(2,1)} %broadcast_in_dim.67), calls=%async_computation | async-start | bytes 2097152 | tf_op jit(solution)/shard_map/all_to_all | solution.py:23
  26.9 27.3 %copy-start = (bf16[3,1,1,256,256]{4,3,2,1,0:T(8,128)(2,1)S(1)}, bf16[3,1,1,256,256]{4,3,2,1,0:T(8,128)(2,1)}, u32[]{:S(2)}) copy-start(bf16[3,1,1,256,256]{4,3,2,1,0:T(8,128)(2,1)} %param.10) | copy-start | bytes 1179652
  26.9 27.3 %copy-start.1 = (f32[3,1,1,64,256]{4,3,2,1,0:T(8,128)S(1)}, f32[3,1,1,64,256]{4,3,2,1,0:T(8,128)}, u32[]{:S(2)}) copy-start(f32[3,1,1,64,256]{4,3,2,1,0:T(8,128)} %param.9) | copy-start | bytes 589828
  30.6 20.9 %collective-permute-start.1 = (bf16[64,256]{1,0:T(8,128)(2,1)S(1)}, bf16[64,256]{1,0:T(8,128)(2,1)S(1)}, u32[]{:S(2)}, u32[]{:S(2)}) collective-permute-start(bf16[64,256]{1,0:T(8,128)(2,1)S(1)} %convert_element_type.159), channel_id=1, source_target_pairs={{0,256},{32,288},{64,320},{96,352},{128,384},{160,416},{192,448},{... | collective-permute-start | bytes 98312 | tf_op jit(solution)/shard_map/ppermute | solution.py:12
  45.5 6.1 %collective-permute-start.2 = (bf16[64,256]{1,0:T(8,128)(2,1)S(1)}, bf16[64,256]{1,0:T(8,128)(2,1)S(1)}, u32[]{:S(2)}, u32[]{:S(2)}) collective-permute-start(bf16[64,256]{1,0:T(8,128)(2,1)S(1)} %convert_element_type.161), channel_id=1, source_target_pairs={{0,480},{32,0},{64,32},{96,64},{128,96},{160,128},{192,160},{224,1... | collective-permute-start | bytes 98312 | tf_op jit(solution)/shard_map/ppermute | solution.py:12
  48.4 5.8 %collective-permute-start = (bf16[64,256]{1,0:T(8,128)(2,1)S(1)}, bf16[64,256]{1,0:T(8,128)(2,1)S(1)}, u32[]{:S(2)}, u32[]{:S(2)}) collective-permute-start(bf16[64,256]{1,0:T(8,128)(2,1)S(1)} %convert_element_type.157), channel_id=1, source_target_pairs={{0,32},{32,64},{64,96},{96,128},{128,160},{160,192},{192,224},{224... | collective-permute-start | bytes 98312 | tf_op jit(solution)/shard_map/ppermute | solution.py:12
  55.5 20.8 %all-to-all-start.1 = ((bf16[32,1,64,256]{3,2,1,0:T(8,128)(2,1)}), bf16[32,1,64,256]{3,2,1,0:T(8,128)(2,1)S(1)}, u32[]{:S(2)}, u32[]{:S(2)}) async-start(bf16[32,1,64,256]{3,2,1,0:T(8,128)(2,1)} %broadcast_in_dim.68), calls=%async_computation.1 | async-start | bytes 2097152 | tf_op jit(solution)/shard_map/all_to_all | solution.py:23
  79.9 14.5 %collective-permute-start.4 = (bf16[64,256]{1,0:T(8,128)(2,1)S(1)}, bf16[64,256]{1,0:T(8,128)(2,1)S(1)}, u32[]{:S(2)}, u32[]{:S(2)}) collective-permute-start(bf16[64,256]{1,0:T(8,128)(2,1)S(1)} %bitcast.224), channel_id=1, source_target_pairs={{0,256},{32,288},{64,320},{96,352},{128,384},{160,416},{192,448},{... | collective-permute-start | bytes 98312 | tf_op jit(solution)/shard_map/ppermute | solution.py:12
  86.2 8.2 %collective-permute-start.5 = (bf16[64,256]{1,0:T(8,128)(2,1)S(1)}, bf16[64,256]{1,0:T(8,128)(2,1)S(1)}, u32[]{:S(2)}, u32[]{:S(2)}) collective-permute-start(bf16[64,256]{1,0:T(8,128)(2,1)S(1)} %bitcast.223), channel_id=1, source_target_pairs={{0,480},{32,0},{64,32},{96,64},{128,96},{160,128},{192,160},{224,1... | collective-permute-start | bytes 98312 | tf_op jit(solution)/shard_map/ppermute | solution.py:12
  91.3 5.8 %collective-permute-start.3 = (bf16[64,256]{1,0:T(8,128)(2,1)S(1)}, bf16[64,256]{1,0:T(8,128)(2,1)S(1)}, u32[]{:S(2)}, u32[]{:S(2)}) collective-permute-start(bf16[64,256]{1,0:T(8,128)(2,1)S(1)} %bitcast.222), channel_id=1, source_target_pairs={{0,32},{32,64},{64,96},{96,128},{128,160},{160,192},{192,224},{224... | collective-permute-start | bytes 98312 | tf_op jit(solution)/shard_map/ppermute | solution.py:12
  134.0 8.8 %collective-permute-start.7 = (bf16[64,256]{1,0:T(8,128)(2,1)S(1)}, bf16[64,256]{1,0:T(8,128)(2,1)S(1)}, u32[]{:S(2)}, u32[]{:S(2)}) collective-permute-start(bf16[64,256]{1,0:T(8,128)(2,1)S(1)} %convert_element_type.180), channel_id=1, source_target_pairs={{0,16},{1,17},{2,18},{3,19},{4,20},{5,21},{6,22},{7,23},{8,24},{9,... | collective-permute-start | bytes 98312 | tf_op jit(solution)/shard_map/ppermute | solution.py:12
  137.4 5.4 %collective-permute-start.8 = (bf16[64,256]{1,0:T(8,128)(2,1)S(1)}, bf16[64,256]{1,0:T(8,128)(2,1)S(1)}, u32[]{:S(2)}, u32[]{:S(2)}) collective-permute-start(bf16[64,256]{1,0:T(8,128)(2,1)S(1)} %convert_element_type.182), channel_id=1, source_target_pairs={{0,31},{1,0},{2,1},{3,2},{4,3},{5,4},{6,5},{7,6},{8,7},{9,8},{10,9... | collective-permute-start | bytes 98312 | tf_op jit(solution)/shard_map/ppermute | solution.py:12
  139.3 8.6 %collective-permute-start.6 = (bf16[64,256]{1,0:T(8,128)(2,1)S(1)}, bf16[64,256]{1,0:T(8,128)(2,1)S(1)}, u32[]{:S(2)}, u32[]{:S(2)}) collective-permute-start(bf16[64,256]{1,0:T(8,128)(2,1)S(1)} %convert_element_type.178), channel_id=1, source_target_pairs={{0,1},{1,2},{2,3},{3,4},{4,5},{5,6},{6,7},{7,8},{8,9},{9,10},{10,1... | collective-permute-start | bytes 98312 | tf_op jit(solution)/shard_map/ppermute | solution.py:12
  181.3 10.8 %collective-permute-start.9 = (bf16[64,256]{1,0:T(8,128)(2,1)S(1)}, bf16[64,256]{1,0:T(8,128)(2,1)S(1)}, u32[]{:S(2)}, u32[]{:S(2)}) collective-permute-start(bf16[64,256]{1,0:T(8,128)(2,1)S(1)} %get-tuple-element.25), channel_id=1, source_target_pairs={{0,1},{1,2},{2,3},{3,4},{4,5},{5,6},{6,7},{7,8},{8,9},{9,10},{10,1... | collective-permute-start | bytes 98312 | tf_op jit(solution)/shard_map/ppermute | solution.py:12
  183.2 8.9 %collective-permute-start.11 = (bf16[64,256]{1,0:T(8,128)(2,1)S(1)}, bf16[64,256]{1,0:T(8,128)(2,1)S(1)}, u32[]{:S(2)}, u32[]{:S(2)}) collective-permute-start(bf16[64,256]{1,0:T(8,128)(2,1)S(1)} %get-tuple-element.26), channel_id=1, source_target_pairs={{0,31},{1,0},{2,1},{3,2},{4,3},{5,4},{6,5},{7,6},{8,7},{9,8},{10,9... | collective-permute-start | bytes 98312 | tf_op jit(solution)/shard_map/ppermute | solution.py:12
  190.2 7.3 %collective-permute-start.10 = (bf16[64,256]{1,0:T(8,128)(2,1)S(1)}, bf16[64,256]{1,0:T(8,128)(2,1)S(1)}, u32[]{:S(2)}, u32[]{:S(2)}) collective-permute-start(bf16[64,256]{1,0:T(8,128)(2,1)S(1)} %get-tuple-element.27), channel_id=1, source_target_pairs={{0,16},{1,17},{2,18},{3,19},{4,20},{5,21},{6,22},{7,23},{8,24},{9,... | collective-permute-start | bytes 98312 | tf_op jit(solution)/shard_map/ppermute | solution.py:12
where the time goes:
time: 199 us; the launch traced here: 198 us
  starting transfers between devices  63.9 us (32%)
  blocking collectives  60.1 us (30%)
  waiting for transfers between devices  44.4 us (22%)
  matrix products  16.8 us (8%)
  local copies, waits for them, and re-layouts  8.54 us (4%)
  other arithmetic  4.13 us (2%)
    all_gather x2, blocking collectives, shards(): gathered_back[current] = lax.all_gather(outgoing, 'row', axis=0, tiled=True)  60.1 us
    ppermute x12, starting transfers between devices, from_behind(): return lax.ppermute(value, axis, pairs)  52.6 us
    all_to_all x2, waiting for transfers between devices, from_everyone(): lax.all_to_all(jnp.broadcast_to(value[None], (count, *value.shape)), axis...  27.4 us
    ppermute x12, waiting for transfers between devices, from_behind(): return lax.ppermute(value, axis, pairs)  17 us
    all_to_all x2, starting transfers between devices, from_everyone(): lax.all_to_all(jnp.broadcast_to(value[None], (count, *value.shape)), axis...  11.4 us
    dot_general x3, matrix products, shards(): jnp.einsum('snb,sab->sna', picked, blocks[pair_idx], preferred_element_ty...  5.58 us
    dot_general x3, matrix products, shards(): jnp.einsum('snb,sba->sna', picked, blocks[pair_idx], preferred_element_ty...  5.14 us
    dot_general x6, matrix products, spread_rows(): jnp.dot(onehot, flattened, precision=lax.Precision.HIGHEST, preferred_ele...  4.19 us
  transfers between devices with their start and end apart: 14, of which 7 were waited for; matrix products, arithmetic and copies ran while one was open for 4% of the time, Pallas kernels for 0%

commit v1 on v0

--- a/solution.py
+++ b/solution.py
@@ -4,6 +4,27 @@
 from jax.sharding import PartitionSpec as P
 
 WINDOW = 2
+
+
+def gather_around(x, axis, dim):
+    length, index, span = (lax.axis_size(axis), lax.axis_index(axis), x.shape[dim])
+    right = [(i, (i + 1) % length) for i in range(length)]
+    backward = [(i, (i - 1) % length) for i in range(length)]
+    whole = jnp.zeros((*x.shape[:dim], length * span, *x.shape[dim + 1 :]), x.dtype)
+    whole = lax.dynamic_update_slice_in_dim(whole, x, index * span, axis=dim)
+    from_left = from_right = x
+    half = length // 2
+    for hop in range(1, half + 1):
+        from_left = lax.ppermute(from_left, axis, right)
+        whole = lax.dynamic_update_slice_in_dim(
+            whole, from_left, (index - hop) % length * span, axis=dim
+        )
+        if hop < length - half:
+            from_right = lax.ppermute(from_right, axis, backward)
+            whole = lax.dynamic_update_slice_in_dim(
+                whole, from_right, (index + hop) % length * span, axis=dim
+            )
+    return whole
 
 
 def from_behind(value, axis, steps):
@@ -140,7 +161,7 @@
         solutions[current] = answer
         if current > 0:
             outgoing = answer.astype(jnp.bfloat16)[None]
-            gathered_back[current] = lax.all_gather(outgoing, "row", axis=0, tiled=True)
+            gathered_back[current] = gather_around(outgoing, "row", 0)
     return jnp.stack(solutions)[:, None, None]
 
 

time: 199 us -> 251 us (1.26)
  the two profiles are of different devices: /device:TPU:32 before, /device:TPU:4 now
where the time goes in v1:
time: 251 us; the launch traced here: 249 us
  starting transfers between devices  168 us (67%)
  waiting for transfers between devices  50.7 us (20%)
  matrix products  16.8 us (7%)
  local copies, waits for them, and re-layouts  8.94 us (4%)
  other arithmetic  3.46 us (1%)
    ppermute x14, starting transfers between devices, gather_around(): from_right = lax.ppermute(from_right, axis, backward)  70.8 us
    ppermute x12, starting transfers between devices, from_behind(): return lax.ppermute(value, axis, pairs)  49.6 us
    ppermute x16, starting transfers between devices, gather_around(): from_left = lax.ppermute(from_left, axis, right)  32 us
    all_to_all x2, waiting for transfers between devices, from_everyone(): lax.all_to_all(jnp.broadcast_to(value[None], (count, *value.shape)), axis...  24.1 us
    ppermute x12, waiting for transfers between devices, from_behind(): return lax.ppermute(value, axis, pairs)  16.4 us
    all_to_all x2, starting transfers between devices, from_everyone(): lax.all_to_all(jnp.broadcast_to(value[None], (count, *value.shape)), axis...  15.4 us
    ppermute x16, waiting for transfers between devices, gather_around(): from_left = lax.ppermute(from_left, axis, right)  10.2 us
    dot_general x3, matrix products, shards(): jnp.einsum('snb,sab->sna', picked, blocks[pair_idx], preferred_element_ty...  5.58 us
  transfers between devices with their start and end apart: 44, of which 9 were waited for; matrix products, arithmetic and copies ran while one was open for 4% of the time, Pallas kernels for 0%

profile of v1, /device:TPU:4, one launch (start us, length us, event | category | flops | bytes accessed | tf_op | source)
XLA Modules:
  0.0 249.2 jit_solution(14433370067061118764)
XLA Ops:
  0.0 1.1 fusion.101
  1.1 1.1 broadcast_in_dim.67
  2.2 9.5 %all-to-all-start = ((bf16[32,1,64,256]{3,2,1,0:T(8,128)(2,1)}), bf16[32,1,64,256]{3,2,1,0:T(8,128)(2,1)S(1)}, u32[]{:S(2)}, u32[]{:S(2)}) async-start(bf16[32,1,64,256]{3,2,1,0:T(8,128)(2,1)} %broadcast_in_dim.67), calls=%async_computation | async-start | bytes 2097152 | tf_op jit(solution)/shard_map/all_to_all | solution.py:44
  13.9 12.7 %all-to-all-done = bf16[32,1,64,256]{3,2,1,0:T(8,128)(2,1)S(1)} async-done(((bf16[32,1,64,256]{3,2,1,0:T(8,128)(2,1)}), bf16[32,1,64,256]{3,2,1,0:T(8,128)(2,1)S(1)}, u32[]{:S(2)}, u32[]{:S(2)}) %all-to-all-start) | async-done | bytes 1048608 | tf_op jit(solution)/shard_map/all_to_all | solution.py:44
  27.1 1.9 fusion.10
  30.8 9.5 %collective-permute-start.2 = (bf16[64,256]{1,0:T(8,128)(2,1)S(1)}, bf16[64,256]{1,0:T(8,128)(2,1)S(1)}, u32[]{:S(2)}, u32[]{:S(2)}) collective-permute-start(bf16[64,256]{1,0:T(8,128)(2,1)S(1)} %convert_element_type.161), channel_id=1, source_target_pairs={{0,480},{32,0},{64,32},{96,64},{128,96},{160,128},{192,160},{224,1... | collective-permute-start | bytes 98312 | tf_op jit(solution)/shard_map/ppermute | solution.py:33
  40.4 6.3 %collective-permute-start.1 = (bf16[64,256]{1,0:T(8,128)(2,1)S(1)}, bf16[64,256]{1,0:T(8,128)(2,1)S(1)}, u32[]{:S(2)}, u32[]{:S(2)}) collective-permute-start(bf16[64,256]{1,0:T(8,128)(2,1)S(1)} %convert_element_type.159), channel_id=1, source_target_pairs={{0,256},{32,288},{64,320},{96,352},{128,384},{160,416},{192,448},{... | collective-permute-start | bytes 98312 | tf_op jit(solution)/shard_map/ppermute | solution.py:33
  46.8 3.8 %collective-permute-start = (bf16[64,256]{1,0:T(8,128)(2,1)S(1)}, bf16[64,256]{1,0:T(8,128)(2,1)S(1)}, u32[]{:S(2)}, u32[]{:S(2)}) collective-permute-start(bf16[64,256]{1,0:T(8,128)(2,1)S(1)} %convert_element_type.157), channel_id=1, source_target_pairs={{0,32},{32,64},{64,96},{96,128},{128,160},{160,192},{192,224},{224... | collective-permute-start | bytes 98312 | tf_op jit(solution)/shard_map/ppermute | solution.py:33
  50.8 4.4 %collective-permute-done.1 = bf16[64,256]{1,0:T(8,128)(2,1)S(1)} collective-permute-done((bf16[64,256]{1,0:T(8,128)(2,1)S(1)}, bf16[64,256]{1,0:T(8,128)(2,1)S(1)}, u32[]{:S(2)}, u32[]{:S(2)}) %collective-permute-start.1) | collective-permute-done | bytes 32800 | tf_op jit(solution)/shard_map/ppermute | solution.py:33
  55.4 1.1 broadcast_in_dim.68
  56.6 5.8 %all-to-all-start.1 = ((bf16[32,1,64,256]{3,2,1,0:T(8,128)(2,1)}), bf16[32,1,64,256]{3,2,1,0:T(8,128)(2,1)S(1)}, u32[]{:S(2)}, u32[]{:S(2)}) async-start(bf16[32,1,64,256]{3,2,1,0:T(8,128)(2,1)} %broadcast_in_dim.68), calls=%async_computation.1 | async-start | bytes 2097152 | tf_op jit(solution)/shard_map/all_to_all | solution.py:44
  63.1 1.8 fusion.6
  65.8 11.4 %all-to-all-done.1 = bf16[32,1,64,256]{3,2,1,0:T(8,128)(2,1)S(1)} async-done(((bf16[32,1,64,256]{3,2,1,0:T(8,128)(2,1)}), bf16[32,1,64,256]{3,2,1,0:T(8,128)(2,1)S(1)}, u32[]{:S(2)}, u32[]{:S(2)}) %all-to-all-start.1) | async-done | bytes 1048608 | tf_op jit(solution)/shard_map/all_to_all | solution.py:44
  77.8 1.8 fusion.2
  79.7 0.8 fusion.18
  80.7 2.8 %collective-permute-start.5 = (bf16[64,256]{1,0:T(8,128)(2,1)S(1)}, bf16[64,256]{1,0:T(8,128)(2,1)S(1)}, u32[]{:S(2)}, u32[]{:S(2)}) collective-permute-start(bf16[64,256]{1,0:T(8,128)(2,1)S(1)} %bitcast.213), channel_id=1, source_target_pairs={{0,480},{32,0},{64,32},{96,64},{128,96},{160,128},{192,160},{224,1... | collective-permute-start | bytes 98312 | tf_op jit(solution)/shard_map/ppermute | solution.py:33
  83.5 6.9 %collective-permute-start.4 = (bf16[64,256]{1,0:T(8,128)(2,1)S(1)}, bf16[64,256]{1,0:T(8,128)(2,1)S(1)}, u32[]{:S(2)}, u32[]{:S(2)}) collective-permute-start(bf16[64,256]{1,0:T(8,128)(2,1)S(1)} %bitcast.214), channel_id=1, source_target_pairs={{0,256},{32,288},{64,320},{96,352},{128,384},{160,416},{192,448},{... | collective-permute-start | bytes 98312 | tf_op jit(solution)/shard_map/ppermute | solution.py:33
  90.5 3.5 %collective-permute-start.3 = (bf16[64,256]{1,0:T(8,128)(2,1)S(1)}, bf16[64,256]{1,0:T(8,128)(2,1)S(1)}, u32[]{:S(2)}, u32[]{:S(2)}) collective-permute-start(bf16[64,256]{1,0:T(8,128)(2,1)S(1)} %bitcast.215), channel_id=1, source_target_pairs={{0,32},{32,64},{64,96},{96,128},{128,160},{160,192},{192,224},{224... | collective-permute-start | bytes 98312 | tf_op jit(solution)/shard_map/ppermute | solution.py:33
  94.0 4.1 %collective-permute-done.4 = bf16[64,256]{1,0:T(8,128)(2,1)S(1)} collective-permute-done((bf16[64,256]{1,0:T(8,128)(2,1)S(1)}, bf16[64,256]{1,0:T(8,128)(2,1)S(1)}, u32[]{:S(2)}, u32[]{:S(2)}) %collective-permute-start.4) | collective-permute-done | bytes 32800 | tf_op jit(solution)/shard_map/ppermute | solution.py:33
  98.5 3.1 %collective-permute-start.6 = (bf16[1,64,256]{2,1,0:T(8,128)(2,1)S(1)}, bf16[1,64,256]{2,1,0:T(8,128)(2,1)S(1)}, u32[]{:S(2)}, u32[]{:S(2)}) collective-permute-start(bf16[1,64,256]{2,1,0:T(8,128)(2,1)S(1)} %get-tuple-element.22), channel_id=1, source_target_pairs={{0,32},{32,64},{64,96},{96,128},{128,160},{160,192},{192,224},{224... | collective-permute-start | bytes 98312 | tf_op jit(solution)/shard_map/ppermute | solution.py:18
  101.6 4.0 %collective-permute-start.7 = (bf16[1,64,256]{2,1,0:T(8,128)(2,1)S(1)}, bf16[1,64,256]{2,1,0:T(8,128)(2,1)S(1)}, u32[]{:S(2)}, u32[]{:S(2)}) collective-permute-start(bf16[1,64,256]{2,1,0:T(8,128)(2,1)S(1)} %get-tuple-element.22), channel_id=1, source_target_pairs={{0,480},{32,0},{64,32},{96,64},{128,96},{160,128},{192,160},{224,1... | collective-permute-start | bytes 98312 | tf_op jit(solution)/shard_map/ppermute | solution.py:23
  105.9 1.9 collective-permute-start.8
  107.8 5.1 %collective-permute-start.9 = (bf16[1,64,256]{2,1,0:T(8,128)(2,1)S(1)}, bf16[1,64,256]{2,1,0:T(8,128)(2,1)S(1)}, u32[]{:S(2)}, u32[]{:S(2)}) collective-permute-start(bf16[1,64,256]{2,1,0:T(8,128)(2,1)S(1)} %collective-permute-done.7), channel_id=1, source_target_pairs={{0,480},{32,0},{64,32},{96,64},{128,96},{160,128},{192,160},{224,1... | collective-permute-start | bytes 98312 | tf_op jit(solution)/shard_map/ppermute | solution.py:23
  113.0 1.9 collective-permute-start.10
  115.0 5.1 %collective-permute-start.11 = (bf16[1,64,256]{2,1,0:T(8,128)(2,1)S(1)}, bf16[1,64,256]{2,1,0:T(8,128)(2,1)S(1)}, u32[]{:S(2)}, u32[]{:S(2)}) collective-permute-start(bf16[1,64,256]{2,1,0:T(8,128)(2,1)S(1)} %collective-permute-done.9), channel_id=1, source_target_pairs={{0,480},{32,0},{64,32},{96,64},{128,96},{160,128},{192,160},{224,1... | collective-permute-start | bytes 98312 | tf_op jit(solution)/shard_map/ppermute | solution.py:23
  120.1 1.9 collective-permute-start.12
  122.1 5.1 %collective-permute-start.13 = (bf16[1,64,256]{2,1,0:T(8,128)(2,1)S(1)}, bf16[1,64,256]{2,1,0:T(8,128)(2,1)S(1)}, u32[]{:S(2)}, u32[]{:S(2)}) collective-permute-start(bf16[1,64,256]{2,1,0:T(8,128)(2,1)S(1)} %collective-permute-done.11), channel_id=1, source_target_pairs={{0,480},{32,0},{64,32},{96,64},{128,96},{160,128},{192,160},{224,1... | collective-permute-start | bytes 98312 | tf_op jit(solution)/shard_map/ppermute | solution.py:23
  127.3 1.9 collective-permute-start.14
  129.2 5.1 %collective-permute-start.15 = (bf16[1,64,256]{2,1,0:T(8,128)(2,1)S(1)}, bf16[1,64,256]{2,1,0:T(8,128)(2,1)S(1)}, u32[]{:S(2)}, u32[]{:S(2)}) collective-permute-start(bf16[1,64,256]{2,1,0:T(8,128)(2,1)S(1)} %collective-permute-done.13), channel_id=1, source_target_pairs={{0,480},{32,0},{64,32},{96,64},{128,96},{160,128},{192,160},{224,1... | collective-permute-start | bytes 98312 | tf_op jit(solution)/shard_map/ppermute | solution.py:23
  134.4 1.9 collective-permute-start.16
  136.3 5.1 %collective-permute-start.17 = (bf16[1,64,256]{2,1,0:T(8,128)(2,1)S(1)}, bf16[1,64,256]{2,1,0:T(8,128)(2,1)S(1)}, u32[]{:S(2)}, u32[]{:S(2)}) collective-permute-start(bf16[1,64,256]{2,1,0:T(8,128)(2,1)S(1)} %collective-permute-done.15), channel_id=1, source_target_pairs={{0,480},{32,0},{64,32},{96,64},{128,96},{160,128},{192,160},{224,1... | collective-permute-start | bytes 98312 | tf_op jit(solution)/shard_map/ppermute | solution.py:23
  141.5 1.9 collective-permute-start.18
  143.5 5.1 %collective-permute-start.19 = (bf16[1,64,256]{2,1,0:T(8,128)(2,1)S(1)}, bf16[1,64,256]{2,1,0:T(8,128)(2,1)S(1)}, u32[]{:S(2)}, u32[]{:S(2)}) collective-permute-start(bf16[1,64,256]{2,1,0:T(8,128)(2,1)S(1)} %collective-permute-done.17), channel_id=1, source_target_pairs={{0,480},{32,0},{64,32},{96,64},{128,96},{160,128},{192,160},{224,1... | collective-permute-start | bytes 98312 | tf_op jit(solution)/shard_map/ppermute | solution.py:23
  148.6 1.9 collective-permute-start.20
  150.6 5.0 %collective-permute-done.20 = bf16[1,64,256]{2,1,0:T(8,128)(2,1)S(1)} collective-permute-done((bf16[1,64,256]{2,1,0:T(8,128)(2,1)S(1)}, bf16[1,64,256]{2,1,0:T(8,128)(2,1)S(1)}, u32[]{:S(2)}, u32[]{:S(2)}) %collective-permute-start.20) | collective-permute-done | bytes 32800 | tf_op jit(solution)/shard_map/ppermute | solution.py:18
  156.2 1.7 fusion
  159.7 1.9 collective-permute-start.23
  161.7 4.4 %collective-permute-start.22 = (bf16[64,256]{1,0:T(8,128)(2,1)S(1)}, bf16[64,256]{1,0:T(8,128)(2,1)S(1)}, u32[]{:S(2)}, u32[]{:S(2)}) collective-permute-start(bf16[64,256]{1,0:T(8,128)(2,1)S(1)} %convert_element_type.180), channel_id=1, source_target_pairs={{0,16},{1,17},{2,18},{3,19},{4,20},{5,21},{6,22},{7,23},{8,24},{9,... | collective-permute-start | bytes 98312 | tf_op jit(solution)/shard_map/ppermute | solution.py:33
  166.1 2.1 collective-permute-start.21
  168.8 1.7 fusion.4
  170.9 2.6 %collective-permute-done.21 = bf16[64,256]{1,0:T(8,128)(2,1)S(1)} collective-permute-done((bf16[64,256]{1,0:T(8,128)(2,1)S(1)}, bf16[64,256]{1,0:T(8,128)(2,1)S(1)}, u32[]{:S(2)}, u32[]{:S(2)}) %collective-permute-start.21) | collective-permute-done | bytes 32800 | tf_op jit(solution)/shard_map/ppermute | solution.py:33
  173.7 2.1 collective-permute-start.24
  176.6 5.1 %collective-permute-start.25 = (bf16[1,64,256]{2,1,0:T(8,128)(2,1)S(1)}, bf16[1,64,256]{2,1,0:T(8,128)(2,1)S(1)}, u32[]{:S(2)}, u32[]{:S(2)}) collective-permute-start(bf16[1,64,256]{2,1,0:T(8,128)(2,1)S(1)} %get-tuple-element.16), channel_id=1, source_target_pairs={{0,480},{32,0},{64,32},{96,64},{128,96},{160,128},{192,160},{224,1... | collective-permute-start | bytes 98312 | tf_op jit(solution)/shard_map/ppermute | solution.py:23
  181.8 1.9 collective-permute-start.26
  183.7 5.1 %collective-permute-start.27 = (bf16[1,64,256]{2,1,0:T(8,128)(2,1)S(1)}, bf16[1,64,256]{2,1,0:T(8,128)(2,1)S(1)}, u32[]{:S(2)}, u32[]{:S(2)}) collective-permute-start(bf16[1,64,256]{2,1,0:T(8,128)(2,1)S(1)} %collective-permute-done.25), channel_id=1, source_target_pairs={{0,480},{32,0},{64,32},{96,64},{128,96},{160,128},{192,160},{224,1... | collective-permute-start | bytes 98312 | tf_op jit(solution)/shard_map/ppermute | solution.py:23
  188.9 1.9 collective-permute-start.28
  190.9 5.1 %collective-permute-start.29 = (bf16[1,64,256]{2,1,0:T(8,128)(2,1)S(1)}, bf16[1,64,256]{2,1,0:T(8,128)(2,1)S(1)}, u32[]{:S(2)}, u32[]{:S(2)}) collective-permute-start(bf16[1,64,256]{2,1,0:T(8,128)(2,1)S(1)} %collective-permute-done.27), channel_id=1, source_target_pairs={{0,480},{32,0},{64,32},{96,64},{128,96},{160,128},{192,160},{224,1... | collective-permute-start | bytes 98312 | tf_op jit(solution)/shard_map/ppermute | solution.py:23
  196.0 1.9 collective-permute-start.30
  198.0 5.1 %collective-permute-start.31 = (bf16[1,64,256]{2,1,0:T(8,128)(2,1)S(1)}, bf16[1,64,256]{2,1,0:T(8,128)(2,1)S(1)}, u32[]{:S(2)}, u32[]{:S(2)}) collective-permute-start(bf16[1,64,256]{2,1,0:T(8,128)(2,1)S(1)} %collective-permute-done.29), channel_id=1, source_target_pairs={{0,480},{32,0},{64,32},{96,64},{128,96},{160,128},{192,160},{224,1... | collective-permute-start | bytes 98312 | tf_op jit(solution)/shard_map/ppermute | solution.py:23
  203.2 1.9 collective-permute-start.32
  205.1 5.1 %collective-permute-start.33 = (bf16[1,64,256]{2,1,0:T(8,128)(2,1)S(1)}, bf16[1,64,256]{2,1,0:T(8,128)(2,1)S(1)}, u32[]{:S(2)}, u32[]{:S(2)}) collective-permute-start(bf16[1,64,256]{2,1,0:T(8,128)(2,1)S(1)} %collective-permute-done.31), channel_id=1, source_target_pairs={{0,480},{32,0},{64,32},{96,64},{128,96},{160,128},{192,160},{224,1... | collective-permute-start | bytes 98312 | tf_op jit(solution)/shard_map/ppermute | solution.py:23
  210.3 1.9 collective-permute-start.34
  212.2 5.1 %collective-permute-start.35 = (bf16[1,64,256]{2,1,0:T(8,128)(2,1)S(1)}, bf16[1,64,256]{2,1,0:T(8,128)(2,1)S(1)}, u32[]{:S(2)}, u32[]{:S(2)}) collective-permute-start(bf16[1,64,256]{2,1,0:T(8,128)(2,1)S(1)} %collective-permute-done.33), channel_id=1, source_target_pairs={{0,480},{32,0},{64,32},{96,64},{128,96},{160,128},{192,160},{224,1... | collective-permute-start | bytes 98312 | tf_op jit(solution)/shard_map/ppermute | solution.py:23
  217.4 1.9 collective-permute-start.36
  219.4 5.3 %collective-permute-start.37 = (bf16[1,64,256]{2,1,0:T(8,128)(2,1)S(1)}, bf16[1,64,256]{2,1,0:T(8,128)(2,1)S(1)}, u32[]{:S(2)}, u32[]{:S(2)}) collective-permute-start(bf16[1,64,256]{2,1,0:T(8,128)(2,1)S(1)} %collective-permute-done.35), channel_id=1, source_target_pairs={{0,480},{32,0},{64,32},{96,64},{128,96},{160,128},{192,160},{224,1... | collective-permute-start | bytes 98312 | tf_op jit(solution)/shard_map/ppermute | solution.py:23
  224.7 1.9 collective-permute-start.38
  226.7 5.0 %collective-permute-done.38 = bf16[1,64,256]{2,1,0:T(8,128)(2,1)S(1)} collective-permute-done((bf16[1,64,256]{2,1,0:T(8,128)(2,1)S(1)}, bf16[1,64,256]{2,1,0:T(8,128)(2,1)S(1)}, u32[]{:S(2)}, u32[]{:S(2)}) %collective-permute-start.38) | collective-permute-done | bytes 32800 | tf_op jit(solution)/shard_map/ppermute | solution.py:18
  232.3 1.7 fusion.8
  234.1 0.8 fusion.22
  235.0 1.9 collective-permute-start.41
  236.9 4.1 %collective-permute-start.40 = (bf16[64,256]{1,0:T(8,128)(2,1)S(1)}, bf16[64,256]{1,0:T(8,128)(2,1)S(1)}, u32[]{:S(2)}, u32[]{:S(2)}) collective-permute-start(bf16[64,256]{1,0:T(8,128)(2,1)S(1)} %get-tuple-element.31), channel_id=1, source_target_pairs={{0,16},{1,17},{2,18},{3,19},{4,20},{5,21},{6,22},{7,23},{8,24},{9,... | collective-permute-start | bytes 98312 | tf_op jit(solution)/shard_map/ppermute | solution.py:33
  241.0 2.1 collective-permute-start.39
  243.2 1.1 collective-permute-done.40
  244.2 4.1 %collective-permute-done.39 = bf16[64,256]{1,0:T(8,128)(2,1)S(1)} collective-permute-done((bf16[64,256]{1,0:T(8,128)(2,1)S(1)}, bf16[64,256]{1,0:T(8,128)(2,1)S(1)}, u32[]{:S(2)}, u32[]{:S(2)}) %collective-permute-start.39) | collective-permute-done | bytes 32800 | tf_op jit(solution)/shard_map/ppermute | solution.py:33
  (127 shorter events, 13.6 us)
Async XLA Ops:
  2.2 24.3 %all-to-all-start = ((bf16[32,1,64,256]{3,2,1,0:T(8,128)(2,1)}), bf16[32,1,64,256]{3,2,1,0:T(8,128)(2,1)S(1)}, u32[]{:S(2)}, u32[]{:S(2)}) async-start(bf16[32,1,64,256]{3,2,1,0:T(8,128)(2,1)} %broadcast_in_dim.67), calls=%async_computation | async-start | bytes 2097152 | tf_op jit(solution)/shard_map/all_to_all | solution.py:44
  27.1 28.2 %copy-start = (bf16[3,1,1,256,256]{4,3,2,1,0:T(8,128)(2,1)S(1)}, bf16[3,1,1,256,256]{4,3,2,1,0:T(8,128)(2,1)}, u32[]{:S(2)}) copy-start(bf16[3,1,1,256,256]{4,3,2,1,0:T(8,128)(2,1)} %param.10) | copy-start | bytes 1179652
  27.1 28.2 %copy-start.1 = (f32[3,1,1,64,256]{4,3,2,1,0:T(8,128)S(1)}, f32[3,1,1,64,256]{4,3,2,1,0:T(8,128)}, u32[]{:S(2)}) copy-start(f32[3,1,1,64,256]{4,3,2,1,0:T(8,128)} %param.9) | copy-start | bytes 589828
  29.1 33.3 %copy-start.2 = (s32[3,1,10]{2,1,0:T(1,128)S(1)}, s32[3,1,10]{2,1,0:T(1,128)}, u32[]{:S(2)}) copy-start(s32[3,1,10]{2,1,0:T(1,128)} %param.12) | copy-start | bytes 364
  30.8 20.0 %collective-permute-start.2 = (bf16[64,256]{1,0:T(8,128)(2,1)S(1)}, bf16[64,256]{1,0:T(8,128)(2,1)S(1)}, u32[]{:S(2)}, u32[]{:S(2)}) collective-permute-start(bf16[64,256]{1,0:T(8,128)(2,1)S(1)} %convert_element_type.161), channel_id=1, source_target_pairs={{0,480},{32,0},{64,32},{96,64},{128,96},{160,128},{192,160},{224,1... | collective-permute-start | bytes 98312 | tf_op jit(solution)/shard_map/ppermute | solution.py:33
  40.4 14.9 %collective-permute-start.1 = (bf16[64,256]{1,0:T(8,128)(2,1)S(1)}, bf16[64,256]{1,0:T(8,128)(2,1)S(1)}, u32[]{:S(2)}, u32[]{:S(2)}) collective-permute-start(bf16[64,256]{1,0:T(8,128)(2,1)S(1)} %convert_element_type.159), channel_id=1, source_target_pairs={{0,256},{32,288},{64,320},{96,352},{128,384},{160,416},{192,448},{... | collective-permute-start | bytes 98312 | tf_op jit(solution)/shard_map/ppermute | solution.py:33
  46.8 8.5 %collective-permute-start = (bf16[64,256]{1,0:T(8,128)(2,1)S(1)}, bf16[64,256]{1,0:T(8,128)(2,1)S(1)}, u32[]{:S(2)}, u32[]{:S(2)}) collective-permute-start(bf16[64,256]{1,0:T(8,128)(2,1)S(1)} %convert_element_type.157), channel_id=1, source_target_pairs={{0,32},{32,64},{64,96},{96,128},{128,160},{160,192},{192,224},{224... | collective-permute-start | bytes 98312 | tf_op jit(solution)/shard_map/ppermute | solution.py:33
  56.6 20.6 %all-to-all-start.1 = ((bf16[32,1,64,256]{3,2,1,0:T(8,128)(2,1)}), bf16[32,1,64,256]{3,2,1,0:T(8,128)(2,1)S(1)}, u32[]{:S(2)}, u32[]{:S(2)}) async-start(bf16[32,1,64,256]{3,2,1,0:T(8,128)(2,1)} %broadcast_in_dim.68), calls=%async_computation.1 | async-start | bytes 2097152 | tf_op jit(solution)/shard_map/all_to_all | solution.py:44
  80.7 13.3 %collective-permute-start.5 = (bf16[64,256]{1,0:T(8,128)(2,1)S(1)}, bf16[64,256]{1,0:T(8,128)(2,1)S(1)}, u32[]{:S(2)}, u32[]{:S(2)}) collective-permute-start(bf16[64,256]{1,0:T(8,128)(2,1)S(1)} %bitcast.213), channel_id=1, source_target_pairs={{0,480},{32,0},{64,32},{96,64},{128,96},{160,128},{192,160},{224,1... | collective-permute-start | bytes 98312 | tf_op jit(solution)/shard_map/ppermute | solution.py:33
  83.5 14.6 %collective-permute-start.4 = (bf16[64,256]{1,0:T(8,128)(2,1)S(1)}, bf16[64,256]{1,0:T(8,128)(2,1)S(1)}, u32[]{:S(2)}, u32[]{:S(2)}) collective-permute-start(bf16[64,256]{1,0:T(8,128)(2,1)S(1)} %bitcast.214), channel_id=1, source_target_pairs={{0,256},{32,288},{64,320},{96,352},{128,384},{160,416},{192,448},{... | collective-permute-start | bytes 98312 | tf_op jit(solution)/shard_map/ppermute | solution.py:33
  90.5 7.7 %collective-permute-start.3 = (bf16[64,256]{1,0:T(8,128)(2,1)S(1)}, bf16[64,256]{1,0:T(8,128)(2,1)S(1)}, u32[]{:S(2)}, u32[]{:S(2)}) collective-permute-start(bf16[64,256]{1,0:T(8,128)(2,1)S(1)} %bitcast.215), channel_id=1, source_target_pairs={{0,32},{32,64},{64,96},{96,128},{128,160},{160,192},{192,224},{224... | collective-permute-start | bytes 98312 | tf_op jit(solution)/shard_map/ppermute | solution.py:33
  98.5 7.4 %collective-permute-start.6 = (bf16[1,64,256]{2,1,0:T(8,128)(2,1)S(1)}, bf16[1,64,256]{2,1,0:T(8,128)(2,1)S(1)}, u32[]{:S(2)}, u32[]{:S(2)}) collective-permute-start(bf16[1,64,256]{2,1,0:T(8,128)(2,1)S(1)} %get-tuple-element.22), channel_id=1, source_target_pairs={{0,32},{32,64},{64,96},{96,128},{128,160},{160,192},{192,224},{224... | collective-permute-start | bytes 98312 | tf_op jit(solution)/shard_map/ppermute | solution.py:18
  101.6 6.2 %collective-permute-start.7 = (bf16[1,64,256]{2,1,0:T(8,128)(2,1)S(1)}, bf16[1,64,256]{2,1,0:T(8,128)(2,1)S(1)}, u32[]{:S(2)}, u32[]{:S(2)}) collective-permute-start(bf16[1,64,256]{2,1,0:T(8,128)(2,1)S(1)} %get-tuple-element.22), channel_id=1, source_target_pairs={{0,480},{32,0},{64,32},{96,64},{128,96},{160,128},{192,160},{224,1... | collective-permute-start | bytes 98312 | tf_op jit(solution)/shard_map/ppermute | solution.py:23
  105.9 7.1 %collective-permute-start.8 = (bf16[1,64,256]{2,1,0:T(8,128)(2,1)S(1)}, bf16[1,64,256]{2,1,0:T(8,128)(2,1)S(1)}, u32[]{:S(2)}, u32[]{:S(2)}) collective-permute-start(bf16[1,64,256]{2,1,0:T(8,128)(2,1)S(1)} %collective-permute-done.6), channel_id=1, source_target_pairs={{0,32},{32,64},{64,96},{96,128},{128,160},{160,192},{192,224},{224... | collective-permute-start | bytes 98312 | tf_op jit(solution)/shard_map/ppermute | solution.py:18
  107.8 7.1 %collective-permute-start.9 = (bf16[1,64,256]{2,1,0:T(8,128)(2,1)S(1)}, bf16[1,64,256]{2,1,0:T(8,128)(2,1)S(1)}, u32[]{:S(2)}, u32[]{:S(2)}) collective-permute-start(bf16[1,64,256]{2,1,0:T(8,128)(2,1)S(1)} %collective-permute-done.7), channel_id=1, source_target_pairs={{0,480},{32,0},{64,32},{96,64},{128,96},{160,128},{192,160},{224,1... | collective-permute-start | bytes 98312 | tf_op jit(solution)/shard_map/ppermute | solution.py:23
  113.0 7.1 %collective-permute-start.10 = (bf16[1,64,256]{2,1,0:T(8,128)(2,1)S(1)}, bf16[1,64,256]{2,1,0:T(8,128)(2,1)S(1)}, u32[]{:S(2)}, u32[]{:S(2)}) collective-permute-start(bf16[1,64,256]{2,1,0:T(8,128)(2,1)S(1)} %collective-permute-done.8), channel_id=1, source_target_pairs={{0,32},{32,64},{64,96},{96,128},{128,160},{160,192},{192,224},{224... | collective-permute-start | bytes 98312 | tf_op jit(solution)/shard_map/ppermute | solution.py:18
  115.0 7.1 %collective-permute-start.11 = (bf16[1,64,256]{2,1,0:T(8,128)(2,1)S(1)}, bf16[1,64,256]{2,1,0:T(8,128)(2,1)S(1)}, u32[]{:S(2)}, u32[]{:S(2)}) collective-permute-start(bf16[1,64,256]{2,1,0:T(8,128)(2,1)S(1)} %collective-permute-done.9), channel_id=1, source_target_pairs={{0,480},{32,0},{64,32},{96,64},{128,96},{160,128},{192,160},{224,1... | collective-permute-start | bytes 98312 | tf_op jit(solution)/shard_map/ppermute | solution.py:23
  120.1 7.1 %collective-permute-start.12 = (bf16[1,64,256]{2,1,0:T(8,128)(2,1)S(1)}, bf16[1,64,256]{2,1,0:T(8,128)(2,1)S(1)}, u32[]{:S(2)}, u32[]{:S(2)}) collective-permute-start(bf16[1,64,256]{2,1,0:T(8,128)(2,1)S(1)} %collective-permute-done.10), channel_id=1, source_target_pairs={{0,32},{32,64},{64,96},{96,128},{128,160},{160,192},{192,224},{224... | collective-permute-start | bytes 98312 | tf_op jit(solution)/shard_map/ppermute | solution.py:18
  122.1 7.1 %collective-permute-start.13 = (bf16[1,64,256]{2,1,0:T(8,128)(2,1)S(1)}, bf16[1,64,256]{2,1,0:T(8,128)(2,1)S(1)}, u32[]{:S(2)}, u32[]{:S(2)}) collective-permute-start(bf16[1,64,256]{2,1,0:T(8,128)(2,1)S(1)} %collective-permute-done.11), channel_id=1, source_target_pairs={{0,480},{32,0},{64,32},{96,64},{128,96},{160,128},{192,160},{224,1... | collective-permute-start | bytes 98312 | tf_op jit(solution)/shard_map/ppermute | solution.py:23
  127.3 7.1 %collective-permute-start.14 = (bf16[1,64,256]{2,1,0:T(8,128)(2,1)S(1)}, bf16[1,64,256]{2,1,0:T(8,128)(2,1)S(1)}, u32[]{:S(2)}, u32[]{:S(2)}) collective-permute-start(bf16[1,64,256]{2,1,0:T(8,128)(2,1)S(1)} %collective-permute-done.12), channel_id=1, source_target_pairs={{0,32},{32,64},{64,96},{96,128},{128,160},{160,192},{192,224},{224... | collective-permute-start | bytes 98312 | tf_op jit(solution)/shard_map/ppermute | solution.py:18
  129.2 7.1 %collective-permute-start.15 = (bf16[1,64,256]{2,1,0:T(8,128)(2,1)S(1)}, bf16[1,64,256]{2,1,0:T(8,128)(2,1)S(1)}, u32[]{:S(2)}, u32[]{:S(2)}) collective-permute-start(bf16[1,64,256]{2,1,0:T(8,128)(2,1)S(1)} %collective-permute-done.13), channel_id=1, source_target_pairs={{0,480},{32,0},{64,32},{96,64},{128,96},{160,128},{192,160},{224,1... | collective-permute-start | bytes 98312 | tf_op jit(solution)/shard_map/ppermute | solution.py:23
  134.4 7.1 %collective-permute-start.16 = (bf16[1,64,256]{2,1,0:T(8,128)(2,1)S(1)}, bf16[1,64,256]{2,1,0:T(8,128)(2,1)S(1)}, u32[]{:S(2)}, u32[]{:S(2)}) collective-permute-start(bf16[1,64,256]{2,1,0:T(8,128)(2,1)S(1)} %collective-permute-done.14), channel_id=1, source_target_pairs={{0,32},{32,64},{64,96},{96,128},{128,160},{160,192},{192,224},{224... | collective-permute-start | bytes 98312 | tf_op jit(solution)/shard_map/ppermute | solution.py:18
  136.3 7.1 %collective-permute-start.17 = (bf16[1,64,256]{2,1,0:T(8,128)(2,1)S(1)}, bf16[1,64,256]{2,1,0:T(8,128)(2,1)S(1)}, u32[]{:S(2)}, u32[]{:S(2)}) collective-permute-start(bf16[1,64,256]{2,1,0:T(8,128)(2,1)S(1)} %collective-permute-done.15), channel_id=1, source_target_pairs={{0,480},{32,0},{64,32},{96,64},{128,96},{160,128},{192,160},{224,1... | collective-permute-start | bytes 98312 | tf_op jit(solution)/shard_map/ppermute | solution.py:23
  141.5 7.1 %collective-permute-start.18 = (bf16[1,64,256]{2,1,0:T(8,128)(2,1)S(1)}, bf16[1,64,256]{2,1,0:T(8,128)(2,1)S(1)}, u32[]{:S(2)}, u32[]{:S(2)}) collective-permute-start(bf16[1,64,256]{2,1,0:T(8,128)(2,1)S(1)} %collective-permute-done.16), channel_id=1, source_target_pairs={{0,32},{32,64},{64,96},{96,128},{128,160},{160,192},{192,224},{224... | collective-permute-start | bytes 98312 | tf_op jit(solution)/shard_map/ppermute | solution.py:18
  143.5 7.1 %collective-permute-start.19 = (bf16[1,64,256]{2,1,0:T(8,128)(2,1)S(1)}, bf16[1,64,256]{2,1,0:T(8,128)(2,1)S(1)}, u32[]{:S(2)}, u32[]{:S(2)}) collective-permute-start(bf16[1,64,256]{2,1,0:T(8,128)(2,1)S(1)} %collective-permute-done.17), channel_id=1, source_target_pairs={{0,480},{32,0},{64,32},{96,64},{128,96},{160,128},{192,160},{224,1... | collective-permute-start | bytes 98312 | tf_op jit(solution)/shard_map/ppermute | solution.py:23
  148.6 7.0 %collective-permute-start.20 = (bf16[1,64,256]{2,1,0:T(8,128)(2,1)S(1)}, bf16[1,64,256]{2,1,0:T(8,128)(2,1)S(1)}, u32[]{:S(2)}, u32[]{:S(2)}) collective-permute-start(bf16[1,64,256]{2,1,0:T(8,128)(2,1)S(1)} %collective-permute-done.18), channel_id=1, source_target_pairs={{0,32},{32,64},{64,96},{96,128},{128,160},{160,192},{192,224},{224... | collective-permute-start | bytes 98312 | tf_op jit(solution)/shard_map/ppermute | solution.py:18
  159.7 11.1 %collective-permute-start.23 = (bf16[64,256]{1,0:T(8,128)(2,1)S(1)}, bf16[64,256]{1,0:T(8,128)(2,1)S(1)}, u32[]{:S(2)}, u32[]{:S(2)}) collective-permute-start(bf16[64,256]{1,0:T(8,128)(2,1)S(1)} %convert_element_type.182), channel_id=1, source_target_pairs={{0,31},{1,0},{2,1},{3,2},{4,3},{5,4},{6,5},{7,6},{8,7},{9,8},{10,9... | collective-permute-start | bytes 98312 | tf_op jit(solution)/shard_map/ppermute | solution.py:33
  161.7 9.2 %collective-permute-start.22 = (bf16[64,256]{1,0:T(8,128)(2,1)S(1)}, bf16[64,256]{1,0:T(8,128)(2,1)S(1)}, u32[]{:S(2)}, u32[]{:S(2)}) collective-permute-start(bf16[64,256]{1,0:T(8,128)(2,1)S(1)} %convert_element_type.180), channel_id=1, source_target_pairs={{0,16},{1,17},{2,18},{3,19},{4,20},{5,21},{6,22},{7,23},{8,24},{9,... | collective-permute-start | bytes 98312 | tf_op jit(solution)/shard_map/ppermute | solution.py:33
  166.1 7.3 %collective-permute-start.21 = (bf16[64,256]{1,0:T(8,128)(2,1)S(1)}, bf16[64,256]{1,0:T(8,128)(2,1)S(1)}, u32[]{:S(2)}, u32[]{:S(2)}) collective-permute-start(bf16[64,256]{1,0:T(8,128)(2,1)S(1)} %convert_element_type.178), channel_id=1, source_target_pairs={{0,1},{1,2},{2,3},{3,4},{4,5},{5,6},{6,7},{7,8},{8,9},{9,10},{10,1... | collective-permute-start | bytes 98312 | tf_op jit(solution)/shard_map/ppermute | solution.py:33
  173.7 8.1 %collective-permute-start.24 = (bf16[1,64,256]{2,1,0:T(8,128)(2,1)S(1)}, bf16[1,64,256]{2,1,0:T(8,128)(2,1)S(1)}, u32[]{:S(2)}, u32[]{:S(2)}) collective-permute-start(bf16[1,64,256]{2,1,0:T(8,128)(2,1)S(1)} %get-tuple-element.16), channel_id=1, source_target_pairs={{0,32},{32,64},{64,96},{96,128},{128,160},{160,192},{192,224},{224... | collective-permute-start | bytes 98312 | tf_op jit(solution)/shard_map/ppermute | solution.py:18
  176.6 7.1 %collective-permute-start.25 = (bf16[1,64,256]{2,1,0:T(8,128)(2,1)S(1)}, bf16[1,64,256]{2,1,0:T(8,128)(2,1)S(1)}, u32[]{:S(2)}, u32[]{:S(2)}) collective-permute-start(bf16[1,64,256]{2,1,0:T(8,128)(2,1)S(1)} %get-tuple-element.16), channel_id=1, source_target_pairs={{0,480},{32,0},{64,32},{96,64},{128,96},{160,128},{192,160},{224,1... | collective-permute-start | bytes 98312 | tf_op jit(solution)/shard_map/ppermute | solution.py:23
  181.8 7.1 %collective-permute-start.26 = (bf16[1,64,256]{2,1,0:T(8,128)(2,1)S(1)}, bf16[1,64,256]{2,1,0:T(8,128)(2,1)S(1)}, u32[]{:S(2)}, u32[]{:S(2)}) collective-permute-start(bf16[1,64,256]{2,1,0:T(8,128)(2,1)S(1)} %collective-permute-done.24), channel_id=1, source_target_pairs={{0,32},{32,64},{64,96},{96,128},{128,160},{160,192},{192,224},{224... | collective-permute-start | bytes 98312 | tf_op jit(solution)/shard_map/ppermute | solution.py:18
  183.7 7.1 %collective-permute-start.27 = (bf16[1,64,256]{2,1,0:T(8,128)(2,1)S(1)}, bf16[1,64,256]{2,1,0:T(8,128)(2,1)S(1)}, u32[]{:S(2)}, u32[]{:S(2)}) collective-permute-start(bf16[1,64,256]{2,1,0:T(8,128)(2,1)S(1)} %collective-permute-done.25), channel_id=1, source_target_pairs={{0,480},{32,0},{64,32},{96,64},{128,96},{160,128},{192,160},{224,1... | collective-permute-start | bytes 98312 | tf_op jit(solution)/shard_map/ppermute | solution.py:23
  188.9 7.1 %collective-permute-start.28 = (bf16[1,64,256]{2,1,0:T(8,128)(2,1)S(1)}, bf16[1,64,256]{2,1,0:T(8,128)(2,1)S(1)}, u32[]{:S(2)}, u32[]{:S(2)}) collective-permute-start(bf16[1,64,256]{2,1,0:T(8,128)(2,1)S(1)} %collective-permute-done.26), channel_id=1, source_target_pairs={{0,32},{32,64},{64,96},{96,128},{128,160},{160,192},{192,224},{224... | collective-permute-start | bytes 98312 | tf_op jit(solution)/shard_map/ppermute | solution.py:18
  190.9 7.1 %collective-permute-start.29 = (bf16[1,64,256]{2,1,0:T(8,128)(2,1)S(1)}, bf16[1,64,256]{2,1,0:T(8,128)(2,1)S(1)}, u32[]{:S(2)}, u32[]{:S(2)}) collective-permute-start(bf16[1,64,256]{2,1,0:T(8,128)(2,1)S(1)} %collective-permute-done.27), channel_id=1, source_target_pairs={{0,480},{32,0},{64,32},{96,64},{128,96},{160,128},{192,160},{224,1... | collective-permute-start | bytes 98312 | tf_op jit(solution)/shard_map/ppermute | solution.py:23
  196.0 7.1 %collective-permute-start.30 = (bf16[1,64,256]{2,1,0:T(8,128)(2,1)S(1)}, bf16[1,64,256]{2,1,0:T(8,128)(2,1)S(1)}, u32[]{:S(2)}, u32[]{:S(2)}) collective-permute-start(bf16[1,64,256]{2,1,0:T(8,128)(2,1)S(1)} %collective-permute-done.28), channel_id=1, source_target_pairs={{0,32},{32,64},{64,96},{96,128},{128,160},{160,192},{192,224},{224... | collective-permute-start | bytes 98312 | tf_op jit(solution)/shard_map/ppermute | solution.py:18
  198.0 7.1 %collective-permute-start.31 = (bf16[1,64,256]{2,1,0:T(8,128)(2,1)S(1)}, bf16[1,64,256]{2,1,0:T(8,128)(2,1)S(1)}, u32[]{:S(2)}, u32[]{:S(2)}) collective-permute-start(bf16[1,64,256]{2,1,0:T(8,128)(2,1)S(1)} %collective-permute-done.29), channel_id=1, source_target_pairs={{0,480},{32,0},{64,32},{96,64},{128,96},{160,128},{192,160},{224,1... | collective-permute-start | bytes 98312 | tf_op jit(solution)/shard_map/ppermute | solution.py:23
  203.2 7.1 %collective-permute-start.32 = (bf16[1,64,256]{2,1,0:T(8,128)(2,1)S(1)}, bf16[1,64,256]{2,1,0:T(8,128)(2,1)S(1)}, u32[]{:S(2)}, u32[]{:S(2)}) collective-permute-start(bf16[1,64,256]{2,1,0:T(8,128)(2,1)S(1)} %collective-permute-done.30), channel_id=1, source_target_pairs={{0,32},{32,64},{64,96},{96,128},{128,160},{160,192},{192,224},{224... | collective-permute-start | bytes 98312 | tf_op jit(solution)/shard_map/ppermute | solution.py:18
  205.1 7.1 %collective-permute-start.33 = (bf16[1,64,256]{2,1,0:T(8,128)(2,1)S(1)}, bf16[1,64,256]{2,1,0:T(8,128)(2,1)S(1)}, u32[]{:S(2)}, u32[]{:S(2)}) collective-permute-start(bf16[1,64,256]{2,1,0:T(8,128)(2,1)S(1)} %collective-permute-done.31), channel_id=1, source_target_pairs={{0,480},{32,0},{64,32},{96,64},{128,96},{160,128},{192,160},{224,1... | collective-permute-start | bytes 98312 | tf_op jit(solution)/shard_map/ppermute | solution.py:23
  210.3 7.2 %collective-permute-start.34 = (bf16[1,64,256]{2,1,0:T(8,128)(2,1)S(1)}, bf16[1,64,256]{2,1,0:T(8,128)(2,1)S(1)}, u32[]{:S(2)}, u32[]{:S(2)}) collective-permute-start(bf16[1,64,256]{2,1,0:T(8,128)(2,1)S(1)} %collective-permute-done.32), channel_id=1, source_target_pairs={{0,32},{32,64},{64,96},{96,128},{128,160},{160,192},{192,224},{224... | collective-permute-start | bytes 98312 | tf_op jit(solution)/shard_map/ppermute | solution.py:18
  212.2 7.1 %collective-permute-start.35 = (bf16[1,64,256]{2,1,0:T(8,128)(2,1)S(1)}, bf16[1,64,256]{2,1,0:T(8,128)(2,1)S(1)}, u32[]{:S(2)}, u32[]{:S(2)}) collective-permute-start(bf16[1,64,256]{2,1,0:T(8,128)(2,1)S(1)} %collective-permute-done.33), channel_id=1, source_target_pairs={{0,480},{32,0},{64,32},{96,64},{128,96},{160,128},{192,160},{224,1... | collective-permute-start | bytes 98312 | tf_op jit(solution)/shard_map/ppermute | solution.py:23
  217.4 7.2 %collective-permute-start.36 = (bf16[1,64,256]{2,1,0:T(8,128)(2,1)S(1)}, bf16[1,64,256]{2,1,0:T(8,128)(2,1)S(1)}, u32[]{:S(2)}, u32[]{:S(2)}) collective-permute-start(bf16[1,64,256]{2,1,0:T(8,128)(2,1)S(1)} %collective-permute-done.34), channel_id=1, source_target_pairs={{0,32},{32,64},{64,96},{96,128},{128,160},{160,192},{192,224},{224... | collective-permute-start | bytes 98312 | tf_op jit(solution)/shard_map/ppermute | solution.py:18
  219.4 7.3 %collective-permute-start.37 = (bf16[1,64,256]{2,1,0:T(8,128)(2,1)S(1)}, bf16[1,64,256]{2,1,0:T(8,128)(2,1)S(1)}, u32[]{:S(2)}, u32[]{:S(2)}) collective-permute-start(bf16[1,64,256]{2,1,0:T(8,128)(2,1)S(1)} %collective-permute-done.35), channel_id=1, source_target_pairs={{0,480},{32,0},{64,32},{96,64},{128,96},{160,128},{192,160},{224,1... | collective-permute-start | bytes 98312 | tf_op jit(solution)/shard_map/ppermute | solution.py:23
  224.7 7.0 %collective-permute-start.38 = (bf16[1,64,256]{2,1,0:T(8,128)(2,1)S(1)}, bf16[1,64,256]{2,1,0:T(8,128)(2,1)S(1)}, u32[]{:S(2)}, u32[]{:S(2)}) collective-permute-start(bf16[1,64,256]{2,1,0:T(8,128)(2,1)S(1)} %collective-permute-done.36), channel_id=1, source_target_pairs={{0,32},{32,64},{64,96},{96,128},{128,160},{160,192},{192,224},{224... | collective-permute-start | bytes 98312 | tf_op jit(solution)/shard_map/ppermute | solution.py:18
  235.0 8.2 %collective-permute-start.41 = (bf16[64,256]{1,0:T(8,128)(2,1)S(1)}, bf16[64,256]{1,0:T(8,128)(2,1)S(1)}, u32[]{:S(2)}, u32[]{:S(2)}) collective-permute-start(bf16[64,256]{1,0:T(8,128)(2,1)S(1)} %get-tuple-element.30), channel_id=1, source_target_pairs={{0,31},{1,0},{2,1},{3,2},{4,3},{5,4},{6,5},{7,6},{8,7},{9,8},{10,9... | collective-permute-start | bytes 98312 | tf_op jit(solution)/shard_map/ppermute | solution.py:33
  236.9 7.3 %collective-permute-start.40 = (bf16[64,256]{1,0:T(8,128)(2,1)S(1)}, bf16[64,256]{1,0:T(8,128)(2,1)S(1)}, u32[]{:S(2)}, u32[]{:S(2)}) collective-permute-start(bf16[64,256]{1,0:T(8,128)(2,1)S(1)} %get-tuple-element.31), channel_id=1, source_target_pairs={{0,16},{1,17},{2,18},{3,19},{4,20},{5,21},{6,22},{7,23},{8,24},{9,... | collective-permute-start | bytes 98312 | tf_op jit(solution)/shard_map/ppermute | solution.py:33
  241.0 7.3 %collective-permute-start.39 = (bf16[64,256]{1,0:T(8,128)(2,1)S(1)}, bf16[64,256]{1,0:T(8,128)(2,1)S(1)}, u32[]{:S(2)}, u32[]{:S(2)}) collective-permute-start(bf16[64,256]{1,0:T(8,128)(2,1)S(1)} %get-tuple-element.29), channel_id=1, source_target_pairs={{0,1},{1,2},{2,3},{3,4},{4,5},{5,6},{6,7},{7,8},{8,9},{9,10},{10,1... | collective-permute-start | bytes 98312 | tf_op jit(solution)/shard_map/ppermute | solution.py:33
